TPU v7x, 512 devices: a whole 4x8x8 slice. The times are simulated.
512 devices in a mesh: dp: 128 (over z, y, core), tensor: 4 (over x).
Axes of the slice: x: 4, y: 8, z: 8, core: 2. Of those that a mesh axis runs over, the one named last changes fastest.
Arguments:
- hidden: bfloat16 [512, 8, 3584], P('dp', None, 'tensor')
- norm_gain: float32 [3584], replicated, may hold values from 0.5 to 2
- head_weight: bfloat16 [152064, 3584], P(('dp', 'tensor'))
- counts: int32 [128], P('dp'), may hold values from 1 to 3, as said below
- destination: int32 [512], P('dp'), may hold values from 0 to 127, as said below
- lengths: int32 [512], P('dp'), may hold values from 1 to 8
- labels: int32 [512, 8], P('dp'), may hold values from 0 to 152063
Outputs:
- scores: float32 [256], P('dp')
Inputs may be any that keep to these rules, and one draw needn't show every extreme that they name: The first counts[i] slots of index i are live; the counts sum to 256. The live slots of index i go to i or to i + 1, lower slots first to i; every index of dp is the destination of exactly 2 live slots; at most 1 live slots of one index go to the next index, a bound reached in every draw; entries of slots that are not live are arbitrary.
All inputs are finite; a program needn't handle non-finite values.
Results may differ from a plain program's by a relative error of at most 0.0025.
Values may be sent and summed in bfloat16 or wider, within the bound.
No kernel may reach another device: no remote copies, remote signals or barrier semaphores. Data moves between devices by JAX's collectives and lax.ppermute only.
A program may use at most 64 MiB of HBM per device.

v0:
```python
import jax
import jax.numpy as jnp
from jax import lax
from jax.sharding import Mesh
from jax.sharding import PartitionSpec as P

BLK_DEV = 2
DP = ("dp_0", "dp_1", "dp_2")
DP_TENSOR = ("dp_0", "dp_1", "dp_2", "tensor")
epsilon = 1e-06


def from_behind(block, axis, distance):
    devices = range(lax.axis_size(axis))
    route = [(i - distance, i) for i in devices if i - distance in devices]
    return lax.ppermute(block, axis, route)


def from_everyone(shard, axis):
    copies = jnp.broadcast_to(shard, (lax.axis_size(axis), *shard.shape))
    return lax.all_to_all(copies, axis, split_axis=0, concat_axis=0, tiled=True)


def in_order(tiles, dim):
    lengths = list(tiles.shape[1:])
    lengths[dim] *= tiles.shape[0]
    return jnp.moveaxis(tiles, 0, dim).reshape(lengths)


def collect(shard, axis, dim):
    tiles = from_everyone(shard, axis)
    return in_order(tiles, dim)


def by_axis(shard, axes):
    for axis in axes:
        shard = lax.pmax(shard, axis)
    return shard


def taken_together(shard, axis):
    return from_everyone(shard, axis).sum(axis=0)


def normalize(rows, norm_gain):
    values = rows.astype(jnp.float32)
    mean_square = jnp.mean(values * values, axis=-1, keepdims=True)
    return (values * lax.rsqrt(mean_square + epsilon) * norm_gain).astype(jnp.bfloat16)


def make_absorb(weight, vocab_start):

    def absorb(running, incoming, offset_row):
        rows, row_labels = incoming
        logits = lax.dot_general(
            rows, weight, (((1,), (1,)), ((), ())), preferred_element_type=jnp.float32
        )
        row_peak = jnp.max(logits, axis=1)
        scaled = jnp.exp(logits - row_peak[:, None])
        vocab_ids = vocab_start + jnp.arange(weight.shape[0], dtype=jnp.int32)
        hit = vocab_ids[None, :] == row_labels[:, None]
        fresh = (
            row_peak,
            jnp.sum(scaled, axis=1),
            jnp.sum(scaled * scaled, axis=1),
            jnp.sum(jnp.where(hit, logits, 0.0), axis=1),
        )
        return tuple((new for new in fresh))

    return absorb


def empty_stats(length):
    return tuple((jnp.zeros((length,), jnp.float32) for index in range(4)))


def earlier_count(flags):
    total = flags.shape[0]
    slot_ids = jnp.arange(total, dtype=jnp.int32)
    before = flags[None, :] & (slot_ids[None, :] < slot_ids[:, None])
    return jnp.sum(before, axis=1)


def per_device(hidden, norm_gain, head_weight, counts, destination, lengths, labels):
    capacity, block_len, quarter_width = hidden.shape
    peer_count = lax.axis_size(DP)
    tensor_ways = lax.axis_size("tensor")
    received_blocks = BLK_DEV
    spill_slots = BLK_DEV - 1
    dp_index = lax.axis_index(DP)
    tensor_index = lax.axis_index("tensor")
    slot_ids = jnp.arange(capacity, dtype=jnp.int32)
    is_live = slot_ids < counts[0]
    leaving = is_live & (destination == dp_index + 1)
    staying = is_live & (destination == dp_index)
    leave_rank = earlier_count(leaving)
    stay_rank = earlier_count(staying)
    flat_hidden = hidden.reshape(capacity, block_len * quarter_width)
    send_pick = (
        jnp.arange(spill_slots, dtype=jnp.int32)[:, None] == leave_rank[None, :]
    ) & leaving[None, :]
    packed = jnp.dot(
        send_pick.astype(jnp.bfloat16), flat_hidden, preferred_element_type=jnp.float32
    ).astype(jnp.bfloat16)
    packed_labels = jnp.sum(jnp.where(send_pick[:, :, None], labels[None, :, :], 0), axis=1)
    packed_lengths = jnp.sum(jnp.where(send_pick, lengths[None, :], 0), axis=1)
    occupied = jnp.sum(send_pick, axis=1)
    arrived, arrived_labels, arrived_lengths, arrived_occupied = from_behind(
        (packed, packed_labels, packed_lengths, occupied), DP, 1
    )
    incoming = jnp.sum(arrived_occupied).astype(jnp.int32)
    final_ids = jnp.arange(received_blocks, dtype=jnp.int32)
    place_in = (final_ids[:, None] == jnp.arange(spill_slots, dtype=jnp.int32)[None, :]) & (
        arrived_occupied > 0
    )[None, :]
    place_own = (final_ids[:, None] == (incoming + stay_rank)[None, :]) & staying[None, :]
    local = jnp.dot(place_in.astype(jnp.bfloat16), arrived, preferred_element_type=jnp.float32)
    local = local + jnp.dot(
        place_own.astype(jnp.bfloat16), flat_hidden, preferred_element_type=jnp.float32
    )
    local = local.astype(jnp.bfloat16).reshape(received_blocks * block_len, quarter_width)
    local_labels = jnp.sum(
        jnp.where(place_in[:, :, None], arrived_labels[None, :, :], 0), axis=1
    ) + jnp.sum(jnp.where(place_own[:, :, None], labels[None, :, :], 0), axis=1)
    local_labels = local_labels.reshape(-1).astype(jnp.int32)
    local_lengths = jnp.sum(jnp.where(place_in, arrived_lengths[None, :], 0), axis=1) + jnp.sum(
        jnp.where(place_own, lengths[None, :], 0), axis=1
    )
    local_lengths = local_lengths.astype(jnp.int32)
    token_count = received_blocks * block_len
    share = token_count // tensor_ways
    vocab_rows = head_weight.shape[0]
    gathered = collect(local, "tensor", 1)
    normed = normalize(gathered, norm_gain)
    absorb = make_absorb(head_weight, (dp_index * tensor_ways + tensor_index) * vocab_rows)
    row_peak, exp_sum, square_sum, label_logit = absorb(
        empty_stats(peer_count * token_count),
        (
            lax.all_gather(normed, DP, axis=0, tiled=True),
            lax.all_gather(local_labels, DP, axis=0, tiled=True),
        ),
        jnp.int32(0),
    )
    global_peak = by_axis(row_peak, DP_TENSOR)
    rescale = jnp.exp(row_peak - global_peak)
    exp_sum, square_sum, label_logit = (
        lax.psum_scatter(exp_sum * rescale, DP_TENSOR, scatter_dimension=0, tiled=True),
        lax.psum_scatter(
            square_sum * rescale * rescale, DP_TENSOR, scatter_dimension=0, tiled=True
        ),
        lax.psum_scatter(label_logit, DP_TENSOR, scatter_dimension=0, tiled=True),
    )
    own_peak = lax.dynamic_slice_in_dim(
        global_peak, (dp_index * tensor_ways + tensor_index) * share, share
    )
    token_error = (
        square_sum / (exp_sum * exp_sum) - 2.0 * jnp.exp(label_logit - own_peak) / exp_sum + 1.0
    )
    position = tensor_index * share + jnp.arange(share, dtype=jnp.int32)
    owner = (
        jnp.arange(received_blocks, dtype=jnp.int32)[:, None] == (position // block_len)[None, :]
    )
    token_length = jnp.sum(jnp.where(owner, local_lengths[:, None], 0), axis=0)
    counted = jnp.where(position % block_len < token_length, token_error, 0.0)
    partial_sum = jnp.sum(jnp.where(owner, counted[None, :], 0.0), axis=1)
    totals = taken_together(partial_sum, "tensor")
    return totals / local_lengths.astype(jnp.float32)


def solution(mesh):
    finer = Mesh(
        mesh.devices.reshape(8, 8, 2, mesh.shape["tensor"]), ("dp_0", "dp_1", "dp_2", "tensor")
    )
    placed = (P(DP, None, "tensor"), P(), P(DP_TENSOR, None), P(DP), P(DP), P(DP), P(DP, None))
    return jax.shard_map(per_device, mesh=finer, in_specs=placed, out_specs=P(DP), check_vma=False)
```

profile of v0, /device:TPU:24, one launch (start us, length us, event | category | flops | bytes accessed | tf_op | source)
XLA Modules:
  0.0 296.8 jit_solution(11436306540069125314)
XLA Ops:
  6.5 0.0 copy-start
  6.5 0.0 copy-start.1
  6.5 0.0 all-gather.2.cloned.1.call-start
  7.4 0.7 compare_and_fusion.3
  8.0 0.1 convert_reduce_fusion.1
  8.1 1.3 select_reduce_fusion.6
  9.4 1.9 collective-permute-start
  11.4 0.8 copy.14
  12.2 0.2 fusion.5
  12.4 4.8 %collective-permute-start.2 = (bf16[1,7168]{1,0:T(2,128)(2,1)S(1)}, bf16[1,7168]{1,0:T(2,128)(2,1)S(1)}, u32[]{:S(2)}, u32[]{:S(2)}) collective-permute-start(bf16[1,7168]{1,0:T(2,128)(2,1)S(1)} %convert_element_type.45), channel_id=1, source_target_pairs={{0,4},{4,8},{8,12},{12,16},{16,20},{20,24},{24,28},{28,32},{32,36}... | collective-permute-start | bytes 43016 | tf_op jit(solution)/shard_map/ppermute | solution.py:16
  17.2 0.1 convert_reduce_fusion
  17.3 0.0 collective-permute-done
  17.3 0.7 broadcast_add_fusion
  18.0 0.8 select_reduce_fusion.5
  19.5 0.0 collective-permute-done.2
  19.6 0.2 add_convert_fusion
  19.8 10.0 %all_to_all.11 = bf16[4,16,896]{2,1,0:T(8,128)(2,1)S(1)} all-to-all(bf16[4,16,896]{2,1,0:T(8,128)(2,1)S(1)} %broadcast_in_dim.150), channel_id=1, replica_groups=mesh['dp_0'=8,'dp_1'=8,'dp_2'=2,'tensor'=4] {'tensor'}, dimensions={0} | all-to-all | bytes 229376 | tf_op jit(solution)/shard_map/all_to_all | solution.py:21
  29.8 0.1 fusion.1
  30.0 1.4 multiply_convert_fusion
  31.4 0.0 all-gather.2.cloned.1.call-update
  31.4 0.8 select_reduce_fusion.2
  32.2 1.9 collective-permute-start.3
  34.1 4.1 %collective-permute-start.1 = (s32[1]{0:T(128)}, s32[1]{0:T(128)}, u32[]{:S(2)}, u32[]{:S(2)}) collective-permute-start(s32[1]{0:T(128)} %bitcast.3), channel_id=1, source_target_pairs={{0,4},{4,8},{8,12},{12,16},{16,20},{20,24},{24,28},{28,32},{32,36}... | collective-permute-start | bytes 20 | tf_op jit(solution)/shard_map/ppermute | solution.py:16
  38.2 1.3 dynamic-slice
  40.2 0.0 copy-done.1
  40.2 0.1 select_reduce_fusion.1
  40.3 0.1 reduce_sum.163
  40.4 0.0 collective-permute-done.1
  40.4 0.6 select_add_fusion
  41.0 0.1 select_reduce_fusion.4
  41.1 0.0 collective-permute-done.3
  41.1 0.1 broadcast_select_fusion
  41.2 0.1 select_n.83
  41.3 0.1 add_dynamic-update-slice_fusion
  41.4 30.5 %all-reduce = s32[2048]{0:T(1024)S(1)} all-reduce(s32[2048]{0:T(1024)S(1)} %add_dynamic-update-slice_fusion), channel_id=1, replica_groups=mesh['dp_0'=8,'dp_1'=8,'dp_2'=2,'tensor'=4] {'dp_0','dp_1','dp_2'}, use_global_device_ids=true, to_apply=%add | all-reduce | flops 2048 | bytes 16384
  71.9 57.0 %all-gather.2.cloned.1.call-done = bf16[2048,3584]{1,0:T(8,128)(2,1)} async-done(((bf16[16,3584]{1,0:T(8,128)(2,1)}), bf16[2048,3584]{1,0:T(8,128)(2,1)}) %all-gather.2.cloned.1.call-update) | async-done | bytes 14680080 | tf_op jit(solution)/shard_map/all_gather | solution.py:139
  128.9 0.0 copy-done
  128.9 9.6 %fusion.9 = (f32[2048]{0:T(1024)S(1)}, f32[2048,297]{0,1:T(8,128)}) fusion(bf16[2048,3584]{1,0:T(8,128)(2,1)} %all-gather.2.cloned.1.call-done, bf16[297,3584]{1,0:T(8,128)(2,1)S(1)} %copy-done), kind=kOutput, calls=%fused_computation.51 | convolution fusion | flops 4360585216 | bytes 19250176 | tf_op jit(solution)/shard_map/dot_general | solution.py:55
  138.5 16.5 %pmax.28 = f32[2048]{0:T(1024)S(1)} all-reduce(f32[2048]{0:T(1024)S(1)} %get-tuple-element.20), channel_id=1, replica_groups=mesh['dp_0'=8,'dp_1'=8,'dp_2'=2,'tensor'=4] {'dp_0'}, use_global_device_ids=true, to_apply=%region_9.10 | all-reduce | flops 2048 | bytes 16384 | tf_op jit(solution)/shard_map/pmax | solution.py:37
  155.0 14.7 %pmax.29 = f32[2048]{0:T(1024)S(1)} all-reduce(f32[2048]{0:T(1024)S(1)} %pmax.28), channel_id=1, replica_groups=mesh['dp_0'=8,'dp_1'=8,'dp_2'=2,'tensor'=4] {'dp_1'}, use_global_device_ids=true, to_apply=%region_10.11 | all-reduce | flops 2048 | bytes 16384 | tf_op jit(solution)/shard_map/pmax | solution.py:37
  169.6 2.5 pmax.30
  172.1 10.5 %pmax.31 = f32[2048]{0:T(1024)S(1)} all-reduce(f32[2048]{0:T(1024)S(1)} %pmax.30), channel_id=1, replica_groups=mesh['dp_0'=8,'dp_1'=8,'dp_2'=2,'tensor'=4] {'tensor'}, use_global_device_ids=true, to_apply=%region_12.13 | all-reduce | flops 2048 | bytes 16384 | tf_op jit(solution)/shard_map/pmax | solution.py:37
  182.7 2.5 fusion
  185.2 94.9 %all-reduce.4 = (f32[2048]{0:T(1024)S(1)}, f32[2048]{0:T(1024)S(1)}, f32[2048]{0:T(1024)S(1)}) all-reduce(f32[2048]{0:T(1024)S(1)} %get-tuple-element.7, f32[2048]{0:T(1024)S(1)} %get-tuple-element.17, f32[2048]{0:T(1024)S(1)} %get-tuple-element.16), channel_id=4, replica_groups=mesh['dp_0'=8,'dp_1'=8,'dp_2'=2,'tensor'=4] {'dp_0','dp_1','dp_2','tensor'}, use_global_device_ids=true, to_apply=%region_19.20.clone | all-reduce | flops 6144 | bytes 49152
  280.1 0.1 compare_select_fusion
  280.2 0.1 select_reduce_fusion.3
  280.3 8.4 %all_to_all.12 = f32[4,1,2]{2,1,0:T(1,128)S(1)} all-to-all(f32[4,1,2]{2,1,0:T(1,128)S(1)} %broadcast_in_dim.163), channel_id=1, replica_groups=mesh['dp_0'=8,'dp_1'=8,'dp_2'=2,'tensor'=4] {'tensor'}, dimensions={0} | all-to-all | bytes 64 | tf_op jit(solution)/shard_map/all_to_all | solution.py:21
  288.8 1.2 convert_divide_fusion
  (16 shorter events, 0.2 us)
Async XLA Ops:
  6.5 122.4 %copy-start = (bf16[297,3584]{1,0:T(8,128)(2,1)S(1)}, bf16[297,3584]{1,0:T(8,128)(2,1)}, u32[]{:S(2)}) copy-start(bf16[297,3584]{1,0:T(8,128)(2,1)} %param.9) | copy-start | bytes 6386692
  6.5 33.7 %copy-start.1 = (s32[4,8]{1,0:T(4,128)S(1)}, s32[4,8]{1,0:T(4,128)}, u32[]{:S(2)}) copy-start(s32[4,8]{1,0:T(4,128)} %param.13) | copy-start | bytes 388
  6.5 122.4 %all-gather.2.cloned.1.call-start = ((), (), s32[]{:S(2)}) async-start(), calls=%async_computation.2 | async-start | bytes 14794752 | tf_op jit(solution)/shard_map/all_gather | solution.py:139
  9.4 7.9 %collective-permute-start = (s32[1]{0:T(128)}, s32[1]{0:T(128)}, u32[]{:S(2)}, u32[]{:S(2)}) collective-permute-start(s32[1]{0:T(128)} %bitcast.1), channel_id=1, source_target_pairs={{0,4},{4,8},{8,12},{12,16},{16,20},{20,24},{24,28},{28,32},{32,36}... | collective-permute-start | bytes 20 | tf_op jit(solution)/shard_map/ppermute | solution.py:16
  12.4 7.1 %collective-permute-start.2 = (bf16[1,7168]{1,0:T(2,128)(2,1)S(1)}, bf16[1,7168]{1,0:T(2,128)(2,1)S(1)}, u32[]{:S(2)}, u32[]{:S(2)}) collective-permute-start(bf16[1,7168]{1,0:T(2,128)(2,1)S(1)} %convert_element_type.45), channel_id=1, source_target_pairs={{0,4},{4,8},{8,12},{12,16},{16,20},{20,24},{24,28},{28,32},{32,36}... | collective-permute-start | bytes 43016 | tf_op jit(solution)/shard_map/ppermute | solution.py:16
  32.2 8.9 %collective-permute-start.3 = (s32[1,8]{1,0:T(1,128)S(1)}, s32[1,8]{1,0:T(1,128)S(1)}, u32[]{:S(2)}, u32[]{:S(2)}) collective-permute-start(s32[1,8]{1,0:T(1,128)S(1)} %bitcast.36), channel_id=1, source_target_pairs={{0,4},{4,8},{8,12},{12,16},{16,20},{20,24},{24,28},{28,32},{32,36}... | collective-permute-start | bytes 104 | tf_op jit(solution)/shard_map/ppermute | solution.py:16
  34.1 6.3 %collective-permute-start.1 = (s32[1]{0:T(128)}, s32[1]{0:T(128)}, u32[]{:S(2)}, u32[]{:S(2)}) collective-permute-start(s32[1]{0:T(128)} %bitcast.3), channel_id=1, source_target_pairs={{0,4},{4,8},{8,12},{12,16},{16,20},{20,24},{24,28},{28,32},{32,36}... | collective-permute-start | bytes 20 | tf_op jit(solution)/shard_map/ppermute | solution.py:16
Sparse Core Ops, SparseCore 0:
  31.6 97.3 all-gather.1
where the time goes:
time: 297 us
  blocking collectives  188 us (63%)
  waiting for transfers between devices  57 us (19%)
  between operations  15.8 us (5%)
  starting transfers between devices  12.7 us (4%)
  other arithmetic  11 us (4%)
  matrix products  9.88 us (3%)
    unnamed x2, blocking collectives  125 us
    all_gather x1, waiting for transfers between devices, per_device(): lax.all_gather(normed, DP, axis=0, tiled=True)  57 us
    pmax x4, blocking collectives, by_axis(): shard = lax.pmax(shard, axis)  44.1 us
    all_to_all x2, blocking collectives, from_everyone(): return lax.all_to_all(copies, axis, split_axis=0, concat_axis=0, tiled=True)  18.4 us
    ppermute x4, starting transfers between devices, from_behind(): return lax.ppermute(block, axis, route)  12.7 us
    dot_general x1, matrix products, absorb(): lax.dot_general(rows, weight, (((1,), (1,)), ((), ())), preferred_element...  9.57 us
  transfers between devices with their start and end apart: 5, of which 1 were waited for; matrix products, arithmetic and copies ran while one was open for 2% of the time, Pallas kernels for 0%

commit v1 on v0

--- a/solution.py
+++ b/solution.py
@@ -136,7 +136,9 @@
     row_peak, exp_sum, square_sum, label_logit = absorb(
         empty_stats(peer_count * token_count),
         (
-            lax.all_gather(normed, DP, axis=0, tiled=True),
+            jnp.concatenate(
+                lax.all_to_all(jnp.stack([normed] * lax.axis_size(DP)), DP, 0, 0), axis=0
+            ),
             lax.all_gather(local_labels, DP, axis=0, tiled=True),
         ),
         jnp.int32(0),

time: 297 us -> 692 us (2.33)
  the two profiles are of different devices: /device:TPU:24 before, /device:TPU:1 now
where the time goes in v1:
time: 692 us
  waiting for transfers between devices  384 us (55%)
  blocking collectives  245 us (35%)
  starting transfers between devices  31.5 us (5%)
  matrix products  9.88 us (1%)
  other arithmetic  9.6 us (1%)
  local copies, waits for them, and re-layouts  9.47 us (1%)
    ppermute x4, waiting for transfers between devices, from_behind(): return lax.ppermute(block, axis, route)  384 us
    unnamed x2, blocking collectives  180 us
    pmax x4, blocking collectives, by_axis(): shard = lax.pmax(shard, axis)  50.6 us
    all_to_all x1, starting transfers between devices, per_device(): lax.all_to_all(jnp.stack([normed] * lax.axis_size(DP)), DP, 0, 0)  19.4 us
    all_to_all x2, blocking collectives, from_everyone(): return lax.all_to_all(copies, axis, split_axis=0, concat_axis=0, tiled=True)  14.1 us
  transfers between devices with their start and end apart: 5, of which 3 were waited for; matrix products, arithmetic and copies ran while one was open for 1% of the time, Pallas kernels for 0%

profile of v1, /device:TPU:1, one launch (start us, length us, event | category | flops | bytes accessed | tf_op | source)
XLA Modules:
  0.0 691.7 jit_solution(9764749307576593477)
XLA Ops:
  0.0 0.0 copy-start
  0.8 0.7 compare_and_fusion.3
  1.5 0.1 convert_reduce_fusion.1
  1.6 1.3 select_reduce_fusion.6
  2.9 4.6 collective-permute-start
  7.5 0.8 copy.14
  8.3 0.2 fusion.5
  8.5 1.9 collective-permute-start.2
  10.4 0.1 convert_reduce_fusion
  10.6 1.3 collective-permute-done
  11.8 0.7 broadcast_add_fusion
  12.5 0.8 select_reduce_fusion.5
  14.0 0.6 collective-permute-done.2
  14.6 0.2 add_convert_fusion
  14.9 7.1 %all_to_all.16 = bf16[4,16,896]{2,1,0:T(8,128)(2,1)S(1)} all-to-all(bf16[4,16,896]{2,1,0:T(8,128)(2,1)S(1)} %broadcast_in_dim.150), channel_id=1, replica_groups=mesh['dp_0'=8,'dp_1'=8,'dp_2'=2,'tensor'=4] {'tensor'}, dimensions={0} | all-to-all | bytes 229376 | tf_op jit(solution)/shard_map/all_to_all | solution.py:21
  22.0 0.1 fusion.1
  22.2 0.8 multiply_convert_fusion
  23.0 7.0 %stack.2 = bf16[128,16,3584]{2,1,0:T(8,128)(2,1)} broadcast(bf16[16,3584]{1,0:T(8,128)(2,1)S(1)} %multiply_convert_fusion), dimensions={1,2} | broadcast | bytes 14794752 | tf_op jit(solution)/shard_map/stack | solution.py:140
  30.0 0.0 copy-start.1
  30.0 19.4 %all-to-all-start.1 = ((bf16[128,16,3584]{2,1,0:T(8,128)(2,1)}), bf16[128,16,3584]{2,1,0:T(8,128)(2,1)}, u32[]{:S(2)}, u32[]{:S(2)}) async-start(bf16[128,16,3584]{2,1,0:T(8,128)(2,1)} %stack.2), calls=%async_computation.1 | async-start | bytes 29360128 | tf_op jit(solution)/shard_map/all_to_all | solution.py:140
  49.5 0.0 copy-done.1
  49.5 0.1 select_reduce_fusion.2
  49.6 3.5 collective-permute-start.3
  53.1 2.0 collective-permute-start.1
  55.2 1.3 dynamic-slice
  57.2 0.1 select_reduce_fusion.1
  57.3 0.1 reduce_sum.163
  57.4 381.8 %collective-permute-done.1 = s32[1]{0:T(128)} collective-permute-done((s32[1]{0:T(128)}, s32[1]{0:T(128)}, u32[]{:S(2)}, u32[]{:S(2)}) %collective-permute-start.1) | collective-permute-done | bytes 36 | tf_op jit(solution)/shard_map/ppermute | solution.py:16
  439.3 0.6 select_add_fusion
  439.9 0.1 select_reduce_fusion.4
  440.0 0.0 collective-permute-done.3
  440.0 0.1 broadcast_select_fusion
  440.0 0.1 select_n.83
  440.1 0.1 add_dynamic-update-slice_fusion
  440.2 83.6 %all-reduce = s32[2048]{0:T(1024)S(1)} all-reduce(s32[2048]{0:T(1024)S(1)} %add_dynamic-update-slice_fusion), channel_id=1, replica_groups=mesh['dp_0'=8,'dp_1'=8,'dp_2'=2,'tensor'=4] {'dp_0','dp_1','dp_2'}, use_global_device_ids=true, to_apply=%add | all-reduce | flops 2048 | bytes 16384
  523.8 0.0 all-to-all-done.1
  523.8 0.0 copy-done
  523.8 9.6 %fusion.9 = (f32[2048]{0:T(1024)S(1)}, f32[2048,297]{0,1:T(8,128)}) fusion(bf16[2048,3584]{1,0:T(8,128)(2,1)} %bitcast.11, bf16[297,3584]{1,0:T(8,128)(2,1)S(1)} %copy-done), kind=kOutput, calls=%fused_computation.51 | convolution fusion | flops 4360585216 | bytes 19250176 | tf_op jit(solution)/shard_map/dot_general | solution.py:55
  533.4 12.3 %pmax.28 = f32[2048]{0:T(1024)S(1)} all-reduce(f32[2048]{0:T(1024)S(1)} %get-tuple-element.20), channel_id=1, replica_groups=mesh['dp_0'=8,'dp_1'=8,'dp_2'=2,'tensor'=4] {'dp_0'}, use_global_device_ids=true, to_apply=%region_9.10 | all-reduce | flops 2048 | bytes 16384 | tf_op jit(solution)/shard_map/pmax | solution.py:37
  545.8 16.7 %pmax.29 = f32[2048]{0:T(1024)S(1)} all-reduce(f32[2048]{0:T(1024)S(1)} %pmax.28), channel_id=1, replica_groups=mesh['dp_0'=8,'dp_1'=8,'dp_2'=2,'tensor'=4] {'dp_1'}, use_global_device_ids=true, to_apply=%region_10.11 | all-reduce | flops 2048 | bytes 16384 | tf_op jit(solution)/shard_map/pmax | solution.py:37
  562.5 14.6 %pmax.30 = f32[2048]{0:T(1024)S(1)} all-reduce(f32[2048]{0:T(1024)S(1)} %pmax.29), channel_id=1, replica_groups=mesh['dp_0'=8,'dp_1'=8,'dp_2'=2,'tensor'=4] {'dp_2'}, use_global_device_ids=true, to_apply=%region_11.12 | all-reduce | flops 2048 | bytes 16384 | tf_op jit(solution)/shard_map/pmax | solution.py:37
  577.1 7.0 %pmax.31 = f32[2048]{0:T(1024)S(1)} all-reduce(f32[2048]{0:T(1024)S(1)} %pmax.30), channel_id=1, replica_groups=mesh['dp_0'=8,'dp_1'=8,'dp_2'=2,'tensor'=4] {'tensor'}, use_global_device_ids=true, to_apply=%region_12.13 | all-reduce | flops 2048 | bytes 16384 | tf_op jit(solution)/shard_map/pmax | solution.py:37
  584.1 2.5 fusion
  586.6 96.8 %all-reduce.4 = (f32[2048]{0:T(1024)S(1)}, f32[2048]{0:T(1024)S(1)}, f32[2048]{0:T(1024)S(1)}) all-reduce(f32[2048]{0:T(1024)S(1)} %get-tuple-element.7, f32[2048]{0:T(1024)S(1)} %get-tuple-element.17, f32[2048]{0:T(1024)S(1)} %get-tuple-element.16), channel_id=4, replica_groups=mesh['dp_0'=8,'dp_1'=8,'dp_2'=2,'tensor'=4] {'dp_0','dp_1','dp_2','tensor'}, use_global_device_ids=true, to_apply=%region_19.20.clone | all-reduce | flops 6144 | bytes 49152
  683.4 0.1 compare_select_fusion
  683.4 0.1 select_reduce_fusion.3
  683.6 7.0 %all_to_all.17 = f32[4,1,2]{2,1,0:T(1,128)S(1)} all-to-all(f32[4,1,2]{2,1,0:T(1,128)S(1)} %broadcast_in_dim.163), channel_id=1, replica_groups=mesh['dp_0'=8,'dp_1'=8,'dp_2'=2,'tensor'=4] {'tensor'}, dimensions={0} | all-to-all | bytes 64 | tf_op jit(solution)/shard_map/all_to_all | solution.py:21
  690.6 1.1 convert_divide_fusion
  (16 shorter events, 0.2 us)
Async XLA Ops:
  0.0 523.8 %copy-start = (bf16[297,3584]{1,0:T(8,128)(2,1)S(1)}, bf16[297,3584]{1,0:T(8,128)(2,1)}, u32[]{:S(2)}) copy-start(bf16[297,3584]{1,0:T(8,128)(2,1)} %param.9) | copy-start | bytes 6386692
  2.9 8.9 %collective-permute-start = (s32[1]{0:T(128)}, s32[1]{0:T(128)}, u32[]{:S(2)}, u32[]{:S(2)}) collective-permute-start(s32[1]{0:T(128)} %bitcast.1), channel_id=1, source_target_pairs={{0,4},{4,8},{8,12},{12,16},{16,20},{20,24},{24,28},{28,32},{32,36}... | collective-permute-start | bytes 20 | tf_op jit(solution)/shard_map/ppermute | solution.py:16
  8.5 6.1 collective-permute-start.2
  30.0 19.5 %copy-start.1 = (s32[4,8]{1,0:T(4,128)S(1)}, s32[4,8]{1,0:T(4,128)}, u32[]{:S(2)}) copy-start(s32[4,8]{1,0:T(4,128)} %param.13) | copy-start | bytes 388
  30.0 493.8 %all-to-all-start.1 = ((bf16[128,16,3584]{2,1,0:T(8,128)(2,1)}), bf16[128,16,3584]{2,1,0:T(8,128)(2,1)}, u32[]{:S(2)}, u32[]{:S(2)}) async-start(bf16[128,16,3584]{2,1,0:T(8,128)(2,1)} %stack.2), calls=%async_computation.1 | async-start | bytes 29360128 | tf_op jit(solution)/shard_map/all_to_all | solution.py:140
  49.6 390.4 %collective-permute-start.3 = (s32[1,8]{1,0:T(1,128)S(1)}, s32[1,8]{1,0:T(1,128)S(1)}, u32[]{:S(2)}, u32[]{:S(2)}) collective-permute-start(s32[1,8]{1,0:T(1,128)S(1)} %bitcast.37), channel_id=1, source_target_pairs={{0,4},{4,8},{8,12},{12,16},{16,20},{20,24},{24,28},{28,32},{32,36}... | collective-permute-start | bytes 104 | tf_op jit(solution)/shard_map/ppermute | solution.py:16
  53.1 386.1 %collective-permute-start.1 = (s32[1]{0:T(128)}, s32[1]{0:T(128)}, u32[]{:S(2)}, u32[]{:S(2)}) collective-permute-start(s32[1]{0:T(128)} %bitcast.3), channel_id=1, source_target_pairs={{0,4},{4,8},{8,12},{12,16},{16,20},{20,24},{24,28},{28,32},{32,36}... | collective-permute-start | bytes 20 | tf_op jit(solution)/shard_map/ppermute | solution.py:16
